TPU v7x, 32 devices: a whole 2x2x4 slice. The times are simulated.
32 devices in a mesh: movie: 16 (over z, y, x), user: 2 (over core).
Axes of the slice: x: 2, y: 2, z: 4, core: 2. Of those that a mesh axis runs over, the one named last changes fastest.
Arguments:
- movie_ids: int32 [128, 128], P(('movie', 'user')), may hold values from 0 to 17919, as said below
- ratings: int32 [128, 128], P(('movie', 'user')), may hold values from 0 to 4
- valid: int32 [128, 128], P(('movie', 'user')), may hold values from 0 to 1, as said below
- weights: bfloat16 [5, 17920, 1024], P(None, 'movie'), may hold values from -0.5 to 0.5
- vis_bias: float32 [5, 17920], P(None, 'movie'), may hold values from -5 to 260
- hid_bias: float32 [1024], replicated, may hold values from -5 to 5
Outputs:
- weight_grad: float32 [5, 17920, 1024], P(None, 'movie')
- visible_grad: float32 [5, 17920], P(None, 'movie')
- hidden_grad: float32 [1024], replicated
- positive_hidden: float32 [128, 1024], P(('movie', 'user'))
Inputs may be any that keep to these rules, and one draw needn't show every extreme that they name: `movie_ids`: movie ids within one user's block are distinct. Of the slots with valid 1 among the users of one device (4 consecutive users), at most 96 name movies of any one block of 1120 consecutive movie ids; in every draw some such block takes exactly 96 from the users of every device. Slots with valid 0 are padding and count nowhere.
All inputs are finite; a program needn't handle non-finite values.
Results may differ from a plain program's by a relative error of at most 0.0054.
Values may be sent and summed in bfloat16 or wider, within the bound.
No kernel may reach another device: no remote copies, remote signals or barrier semaphores. Data moves between devices by JAX's collectives and lax.ppermute only.
A program may use at most 128 MiB of HBM per device.

v0:
```python
import jax
import jax.numpy as jnp
from jax import lax
from jax.sharding import PartitionSpec as P


def reconstruct(hidden_rows, weight_table, bias_row, rated_mask, levels):
    group_rows = hidden_rows.shape[0]
    rating_logits = (
        lax.dot_general(
            hidden_rows, weight_table, (((1,), (1,)), ((), ())), preferred_element_type=jnp.float32
        )
        + bias_row[None, :]
    )
    shaped = rating_logits.reshape(group_rows, levels, -1)
    largest = jnp.max(shaped, axis=1, keepdims=True)
    exponent = jnp.exp(shaped - largest)
    softened = (exponent / jnp.sum(exponent, axis=1, keepdims=True)).astype(jnp.bfloat16)
    return (softened * rated_mask[:, None, :]).reshape(group_rows, -1)


def hidden_phase(visible, weight_table, hid_bias, local_users, device_index):
    combined = jnp.dot(visible, weight_table, preferred_element_type=jnp.float32)
    all_probs = jax.nn.sigmoid(hid_bias[None, :] + lax.psum(combined, "movie"))
    own_rows = lax.dynamic_slice_in_dim(all_probs, device_index * local_users, local_users, 0)
    return (own_rows, all_probs.astype(jnp.bfloat16))


def on_device(movie_ids, ratings, valid, weights, vis_bias, hid_bias):
    owners = lax.axis_size("movie")
    device_index = lax.axis_index("movie")
    local_users, slot_count = movie_ids.shape
    levels, local_movies, hidden = weights.shape
    columns = levels * local_movies
    group_rows = owners * local_users
    capacity = max(2, 3 * local_users * slot_count // owners)
    flat_ids = movie_ids.reshape(-1)
    owner_ids = flat_ids // local_movies
    column_ids = ratings.reshape(-1) * local_movies + flat_ids % local_movies
    user_ids = jnp.arange(local_users * slot_count, dtype=jnp.int32) // slot_count
    usable = valid.reshape(-1) == 1
    matches = (owner_ids[:, None] == jnp.arange(owners, dtype=jnp.int32)[None, :]) & usable[:, None]
    ranking = jnp.cumsum(matches.astype(jnp.int32), axis=0) - 1
    placed = jnp.sum(jnp.where(matches, ranking, 0), axis=1)
    target = jnp.where(usable, owner_ids, owners)
    user_slots = (
        jnp.zeros((owners, capacity), jnp.int32).at[target, placed].set(user_ids, mode="drop")
    )
    column_slots = (
        jnp.full((owners, capacity), -1, jnp.int32).at[target, placed].set(column_ids, mode="drop")
    )
    got_users, got_columns = (
        lax.all_to_all(user_slots, "movie", split_axis=0, concat_axis=0, tiled=True),
        lax.all_to_all(column_slots, "movie", split_axis=0, concat_axis=0, tiled=True),
    )
    user_hot = (got_users[:, :, None] == jnp.arange(local_users, dtype=jnp.int32)).astype(
        jnp.bfloat16
    )
    column_hot = (got_columns[:, :, None] == jnp.arange(columns, dtype=jnp.int32)).astype(
        jnp.bfloat16
    )
    shown = jnp.einsum("ncu,ncj->nuj", user_hot, column_hot, preferred_element_type=jnp.float32)
    shown = shown.reshape(group_rows, columns).astype(jnp.bfloat16)
    rated_mask = jnp.sum(shown.reshape(group_rows, levels, local_movies), axis=1)
    weight_table = weights.reshape(columns, hidden)
    positive_own, positive_group = hidden_phase(
        shown, weight_table, hid_bias, local_users, device_index
    )
    reconstructed_ratings = reconstruct(
        positive_group, weight_table, vis_bias.reshape(columns), rated_mask, levels
    )
    negative_own, negative_group = hidden_phase(
        reconstructed_ratings, weight_table, hid_bias, local_users, device_index
    )
    contract = (((0,), (0,)), ((), ()))
    weight_grad = lax.dot_general(
        shown, positive_group, contract, preferred_element_type=jnp.float32
    )
    weight_grad = weight_grad - lax.dot_general(
        reconstructed_ratings, negative_group, contract, preferred_element_type=jnp.float32
    )
    visible_grad = jnp.sum(shown.astype(jnp.float32), axis=0) - jnp.sum(
        reconstructed_ratings.astype(jnp.float32), axis=0
    )
    weight_grad, visible_grad = lax.psum((weight_grad, visible_grad), "user")
    hidden_grad = lax.psum(jnp.sum(positive_own - negative_own, axis=0), ("movie", "user"))
    return (
        weight_grad.reshape(levels, local_movies, hidden),
        visible_grad.reshape(levels, local_movies),
        hidden_grad,
        positive_own,
    )


def solution(mesh):
    in_specs = (
        P(("movie", "user"), None),
        P(("movie", "user"), None),
        P(("movie", "user"), None),
        P(None, "movie", None),
        P(None, "movie"),
        P(),
    )
    out_specs = (P(None, "movie", None), P(None, "movie"), P(), P(("movie", "user"), None))
    return jax.shard_map(
        on_device, mesh=mesh, in_specs=in_specs, out_specs=out_specs, check_vma=False
    )
```

profile of v0, /device:TPU:0, one launch (start us, length us, event | category | flops | bytes accessed | tf_op | source)
XLA Modules:
  0.0 498.8 jit_solution(16229236096760497218)
XLA Ops:
  7.2 0.7 fusion.32
  7.9 0.7 fusion.31
  8.5 0.7 broadcast_compare_fusion
  9.2 0.7 add_select_fusion.2
  9.9 0.7 fusion.18
  10.7 1.2 reduce-window.6
  11.8 0.2 slice_reduce_fusion
  12.1 0.1 fusion.12
  12.2 0.6 broadcast_in_dim.15
  12.8 70.4 %scatter_fusion.1 = s32[16,96]{1,0:T(8,128)} fusion(s32[16,96]{1,0:T(8,128)} %broadcast_in_dim.15, s32[512]{0:T(512)S(1)} %bitcast.81, s32[512]{0:T(512)S(1)} %get-tuple-element.10), kind=kCustom, calls=%fused_computation.1 | custom fusion | bytes 10240 | tf_op jit(solution)/shard_map/scatter | solution.py:50
  83.2 8.4 %all-to-all-start.1 = ((s32[16,1,96]{2,1,0:T(1,128)}), s32[16,1,96]{2,1,0:T(1,128)S(1)}, u32[]{:S(2)}, u32[]{:S(2)}) async-start(s32[16,1,96]{2,1,0:T(1,128)} %bitcast.13), calls=%async_computation.1 | async-start | bytes 16384 | tf_op jit(solution)/shard_map/all_to_all | solution.py:54
  91.6 0.0 all-reduce.4.cloned.1.call-start
  91.7 25.2 %scatter_fusion = s32[16,96]{1,0:T(8,128)S(1)} fusion(s32[16,96]{1,0:T(8,128)S(1)} %broadcast_in_dim.12, s32[512]{0:T(512)S(1)} %bitcast.82, s32[512]{0:T(512)S(1)} %add_select_fusion.1), kind=kCustom, calls=%fused_computation | custom fusion | bytes 10240 | tf_op jit(solution)/shard_map/scatter | solution.py:47
  116.8 0.0 all-to-all-done.1
  116.9 14.0 %all_to_all.18 = s32[16,1,96]{2,1,0:T(1,128)S(1)} all-to-all(s32[16,1,96]{2,1,0:T(1,128)S(1)} %bitcast.75), channel_id=1, replica_groups=mesh['movie'=16,'user'=2] {'movie'}, dimensions={0} | all-to-all | bytes 12288 | tf_op jit(solution)/shard_map/all_to_all | solution.py:53
  130.9 6.6 %convert_reduce_fusion.1 = (f32[5600]{0:T(1024)S(1)}, bf16[16,4,5600]{2,1,0:T(4,128)(2,1)S(1)}) fusion(s32[16,96]{1,0:T(8,128)S(1)} %bitcast.85, s32[16,96]{1,0:T(8,128)S(1)} %bitcast.86), kind=kOutput, calls=%fused_computation.12 | convolution fusion | flops 78490144 | bytes 751488 | tf_op jit(solution)/shard_map/ncu,ncj->nuj/dot_general | solution.py:62
  137.5 0.3 convert_element_type.42
  137.8 0.0 copy-start.1
  137.8 0.0 copy-start.3
  137.8 7.3 %fusion.24 = f32[64,1024]{1,0:T(8,128)} fusion(bf16[64,5600]{1,0:T(8,128)(2,1)S(1)} %convert_element_type.42, bf16[5600,1024]{1,0:T(8,128)(2,1)} %bitcast.77), kind=kOutput, calls=%fused_computation.65 | convolution fusion | flops 734003200 | bytes 12447744 | tf_op jit(solution)/shard_map/dot_general | solution.py:23
  145.1 0.0 copy-done.1
  145.1 0.0 all-reduce.4.cloned.1.call-update
  145.2 0.2 all-reduce.6.cloned.1.call-start
  145.4 0.0 copy-done.3
  145.4 0.1 add.98
  145.5 0.9 convert_element_type.45
  146.4 0.0 copy-start.4
  146.4 0.8 reduce_sum.62
  147.2 1.1 mul.26
  148.3 2.7 mul.27
  151.1 98.4 %all-reduce.4.cloned.1.call-done = f32[64,1024]{1,0:T(8,128)} async-done(((f32[64,1024]{1,0:T(8,128)}), f32[64,1024]{1,0:T(8,128)}) %all-reduce.4.cloned.1.call-update) | async-done | bytes 262160 | tf_op jit(solution)/shard_map/psum | solution.py:24
  249.4 0.0 copy-done.4
  249.4 1.0 add_divide_fusion.1
  250.5 0.0 slice-start.1
  250.5 0.0 slice-start.2
  250.5 11.1 %fusion.9 = f32[5600,1024]{1,0:T(8,128)} fusion(bf16[64,5600]{1,0:T(8,128)(2,1)} %copy-done.1, f32[64,1024]{1,0:T(8,128)S(1)} %add_divide_fusion.1), kind=kOutput, calls=%fused_computation.22 | convolution fusion | flops 734068736 | bytes 23916544 | tf_op jit(solution)/shard_map/dot_general | solution.py:76
  261.7 0.0 slice-done
  261.7 0.0 slice-done.1
  261.7 0.0 slice-done.2
  261.7 4.7 convolution_add_fusion
  266.4 1.9 reshape.182
  268.3 0.7 reduce_max.9
  269.0 1.0 fusion.3
  270.0 0.8 fusion.4
  270.8 7.1 %convolution_bitcast_fusion = f32[64,1024]{1,0:T(8,128)} fusion(bf16[5,1120,1024]{2,1,0:T(8,128)(2,1)} %param.9, bf16[64,5,1120]{2,1,0:T(8,128)(2,1)S(1)} %fusion.4), kind=kOutput, calls=%fused_computation.15 | convolution fusion | flops 734003200 | bytes 12447744 | tf_op jit(solution)/shard_map/dot_general | solution.py:23
  277.9 0.0 all-reduce.6.cloned.1.call-update
  277.9 0.3 all-reduce.8.cloned.1.call-start
  278.2 0.2 sub.51
  278.3 1.6 sub.52
  280.0 1.6 div.54
  281.5 3.0 div.55
  284.5 0.0 copy-done
  284.5 0.0 copy-done.2
  284.5 3.0 convert_reduce_fusion
  287.5 97.3 %all-reduce.6.cloned.1.call-done = f32[64,1024]{1,0:T(8,128)} async-done(((f32[64,1024]{1,0:T(8,128)}), f32[64,1024]{1,0:T(8,128)}) %all-reduce.6.cloned.1.call-update) | async-done | bytes 262160 | tf_op jit(solution)/shard_map/psum | solution.py:24
  384.8 1.0 add_divide_fusion
  385.8 15.5 %convolution_subtract_fusion = f32[5600,1024]{1,0:T(8,128)} fusion(f32[5600,1024]{1,0:T(8,128)} %fusion.9, bf16[64,5600]{1,0:T(8,128)(2,1)} %get-tuple-element.7, f32[64,1024]{1,0:T(8,128)S(1)} %add_divide_fusion), kind=kOutput, calls=%fused_computation.5 | convolution fusion | flops 739803136 | bytes 46854144 | tf_op jit(solution)/shard_map/dot_general | solution.py:79
  401.3 0.0 all-reduce.8.cloned.1.call-update
  401.3 0.1 reshape.184
  401.4 4.0 psum.38
  405.5 0.6 subtract_reduce_fusion
  406.1 39.4 %psum.39 = f32[1024]{0:T(1024)} all-reduce(f32[1024]{0:T(1024)S(1)} %get-tuple-element.4), channel_id=1, replica_groups=mesh['movie'=16,'user'=2] {'movie','user'}, use_global_device_ids=true, to_apply=%region_15.16 | all-reduce | flops 1024 | bytes 8192 | tf_op jit(solution)/shard_map/psum | solution.py:86
  445.4 30.3 %all-reduce.8.cloned.1.call-done = f32[5,1120,1024]{2,1,0:T(8,128)} async-done(((f32[5,1120,1024]{2,1,0:T(8,128)}), f32[5,1120,1024]{2,1,0:T(8,128)}) %all-reduce.8.cloned.1.call-update) | async-done | bytes 22937616 | tf_op jit(solution)/shard_map/psum | solution.py:85
  475.8 16.5 %copy.37 = f32[5,1120,1024]{2,1,0:T(8,128)} copy(f32[5,1120,1024]{2,1,0:T(8,128)} %all-reduce.8.cloned.1.call-done) | data formatting | bytes 45875200
  (11 shorter events, 0.1 us)
Async XLA Ops:
  83.2 33.7 %all-to-all-start.1 = ((s32[16,1,96]{2,1,0:T(1,128)}), s32[16,1,96]{2,1,0:T(1,128)S(1)}, u32[]{:S(2)}, u32[]{:S(2)}) async-start(s32[16,1,96]{2,1,0:T(1,128)} %bitcast.13), calls=%async_computation.1 | async-start | bytes 16384 | tf_op jit(solution)/shard_map/all_to_all | solution.py:54
  91.6 157.9 %all-reduce.4.cloned.1.call-start = ((), (), s32[]{:S(2)}) async-start(), calls=%async_computation.2 | async-start | bytes 524288 | tf_op jit(solution)/shard_map/psum | solution.py:24
  137.8 7.4 %copy-start.1 = (bf16[64,5600]{1,0:T(8,128)(2,1)}, bf16[64,5600]{1,0:T(8,128)(2,1)S(1)}, u32[]{:S(2)}) copy-start(bf16[64,5600]{1,0:T(8,128)(2,1)S(1)} %convert_element_type.42) | copy-start | bytes 2150404
  137.8 7.6 %copy-start.3 = (f32[5,1120]{1,0:T(8,128)S(1)}, f32[5,1120]{1,0:T(8,128)}, u32[]{:S(2)}) copy-start(f32[5,1120]{1,0:T(8,128)} %param.10) | copy-start | bytes 67204
  145.2 239.6 %all-reduce.6.cloned.1.call-start = ((), (), s32[]{:S(2)}) async-start(), calls=%async_computation.3 | async-start | bytes 524288 | tf_op jit(solution)/shard_map/psum | solution.py:24
  146.4 103.1 %copy-start.4 = (f32[1024]{0:T(1024)S(1)}, f32[1024]{0:T(1024)}, u32[]{:S(2)}) copy-start(f32[1024]{0:T(1024)} %param.11) | copy-start | bytes 12292
  148.3 113.3 %slice-start = ((s8[11468800]{0:T(1024)(128)(4,1)}), s8[3080192]{0:T(1024)(128)(4,1)S(1)}, s32[]{:S(2)}) async-start(s8[11468800]{0:T(1024)(128)(4,1)} %bitcast.78), calls=%async_computation.5 | async-start | bytes 6160384
  250.5 11.2 %slice-start.1 = ((s8[11468800]{0:T(1024)(128)(4,1)}), s8[4194304]{0:T(1024)(128)(4,1)S(1)}, s32[]{:S(2)}) async-start(s8[11468800]{0:T(1024)(128)(4,1)} %bitcast.78), calls=%async_computation.6 | async-start | bytes 8388608
  250.5 11.2 %slice-start.2 = ((s8[11468800]{0:T(1024)(128)(4,1)}), s8[4194304]{0:T(1024)(128)(4,1)S(1)}, s32[]{:S(2)}) async-start(s8[11468800]{0:T(1024)(128)(4,1)} %bitcast.78), calls=%async_computation.7 | async-start | bytes 8388608
  277.9 197.9 %all-reduce.8.cloned.1.call-start = ((), (), s32[]{:S(2)}) async-start(), calls=%async_computation.4 | async-start | bytes 45875200 | tf_op jit(solution)/shard_map/psum | solution.py:85
  281.5 3.0 copy-start
  281.5 3.0 copy-start.2
Sparse Core Ops, SparseCore 0:
  145.3 104.1 all-reduce.3
  278.0 106.6 all-reduce.5
  401.4 74.2 all-reduce.7
where the time goes:
time: 501 us; the launch traced here: 499 us
  waiting for transfers between devices  226 us (45%)
  local copies, waits for them, and re-layouts  126 us (25%)
  blocking collectives  57.4 us (11%)
  matrix products  52.3 us (10%)
  between operations  14 us (3%)
  other arithmetic  13.7 us (3%)
  starting transfers between devices  8.93 us (2%)
    psum x2, waiting for transfers between devices, hidden_phase(): all_probs = jax.nn.sigmoid(hid_bias[None, :] + lax.psum(combined, 'movie'))  196 us
    scatter x1, local copies, waits for them, and re-layouts, on_device(): jnp.full((owners, capacity), -1, jnp.int32).at[target, placed]  70.4 us
    psum x1, blocking collectives, on_device(): lax.psum(jnp.sum(positive_own - negative_own, axis=0), ('movie', 'user'))  39.4 us
    psum x1, waiting for transfers between devices, on_device(): weight_grad, visible_grad = lax.psum((weight_grad, visible_grad), 'user')  30.3 us
    scatter x1, local copies, waits for them, and re-layouts, on_device(): jnp.zeros((owners, capacity), jnp.int32).at[target, placed]  25.2 us
    unnamed x17, local copies, waits for them, and re-layouts  16.6 us
    dot_general x1, matrix products, on_device(): lax.dot_general(reconstructed_ratings, negative_group, contract, preferre...  15.5 us
    dot_general x2, matrix products, hidden_phase(): jnp.dot(visible, weight_table, preferred_element_type=jnp.float32)  14.4 us
  transfers between devices with their start and end apart: 4, of which 3 were waited for; matrix products, arithmetic and copies ran while one was open for 8% of the time, Pallas kernels for 0%

commit v1 on v0

--- a/solution.py
+++ b/solution.py
@@ -83,7 +83,9 @@
         reconstructed_ratings.astype(jnp.float32), axis=0
     )
     weight_grad, visible_grad = lax.psum((weight_grad, visible_grad), "user")
-    hidden_grad = lax.psum(jnp.sum(positive_own - negative_own, axis=0), ("movie", "user"))
+    payload = jnp.sum(positive_own - negative_own, axis=0)
+    everything = jax.lax.all_gather(payload, ("movie", "user"))
+    hidden_grad = jnp.sum(everything, 0)
     return (
         weight_grad.reshape(levels, local_movies, hidden),
         visible_grad.reshape(levels, local_movies),

time: 501 us -> 501 us (level)
    all_gather x0 -> x1, blocking collectives: none -> 39.9 us  [on_device(): everything = jax.lax.all_gather(payload, ('movie', 'user'))]
    psum x1 -> x0, blocking collectives: 39.4 us -> none  [on_device(): lax.psum(jnp.sum(positive_own - negative_own, axis=0), ('movie', 'user'))]
where the time goes in v1:
time: 501 us; the launch traced here: 499 us
  waiting for transfers between devices  225 us (45%)
  local copies, waits for them, and re-layouts  126 us (25%)
  blocking collectives  57.9 us (12%)
  matrix products  52.3 us (10%)
  other arithmetic  14.3 us (3%)
  between operations  14 us (3%)
  starting transfers between devices  8.93 us (2%)
    psum x2, waiting for transfers between devices, hidden_phase(): all_probs = jax.nn.sigmoid(hid_bias[None, :] + lax.psum(combined, 'movie'))  196 us
    scatter x1, local copies, waits for them, and re-layouts, on_device(): jnp.full((owners, capacity), -1, jnp.int32).at[target, placed]  70.4 us
    all_gather x1, blocking collectives, on_device(): everything = jax.lax.all_gather(payload, ('movie', 'user'))  39.9 us
    psum x1, waiting for transfers between devices, on_device(): weight_grad, visible_grad = lax.psum((weight_grad, visible_grad), 'user')  29.2 us
    scatter x1, local copies, waits for them, and re-layouts, on_device(): jnp.zeros((owners, capacity), jnp.int32).at[target, placed]  25.2 us
    unnamed x17, local copies, waits for them, and re-layouts  16.6 us
    dot_general x1, matrix products, on_device(): lax.dot_general(reconstructed_ratings, negative_group, contract, preferre...  15.5 us
    dot_general x2, matrix products, hidden_phase(): jnp.dot(visible, weight_table, preferred_element_type=jnp.float32)  14.4 us
  transfers between devices with their start and end apart: 4, of which 3 were waited for; matrix products, arithmetic and copies ran while one was open for 8% of the time, Pallas kernels for 0%

profile of v1, /device:TPU:0, one launch (start us, length us, event | category | flops | bytes accessed | tf_op | source)
XLA Modules:
  0.0 498.8 jit_solution(16024511404043122188)
XLA Ops:
  7.2 0.7 fusion.32
  7.9 0.7 fusion.31
  8.5 0.7 broadcast_compare_fusion
  9.2 0.7 add_select_fusion.2
  9.9 0.7 fusion.18
  10.7 1.2 reduce-window.6
  11.8 0.2 slice_reduce_fusion
  12.1 0.1 fusion.12
  12.2 0.6 broadcast_in_dim.15
  12.8 70.4 %scatter_fusion.1 = s32[16,96]{1,0:T(8,128)} fusion(s32[16,96]{1,0:T(8,128)} %broadcast_in_dim.15, s32[512]{0:T(512)S(1)} %bitcast.81, s32[512]{0:T(512)S(1)} %get-tuple-element.10), kind=kCustom, calls=%fused_computation.1 | custom fusion | bytes 10240 | tf_op jit(solution)/shard_map/scatter | solution.py:50
  83.2 8.4 %all-to-all-start.1 = ((s32[16,1,96]{2,1,0:T(1,128)}), s32[16,1,96]{2,1,0:T(1,128)S(1)}, u32[]{:S(2)}, u32[]{:S(2)}) async-start(s32[16,1,96]{2,1,0:T(1,128)} %bitcast.13), calls=%async_computation.1 | async-start | bytes 16384 | tf_op jit(solution)/shard_map/all_to_all | solution.py:54
  91.6 0.0 all-reduce.4.cloned.1.call-start
  91.7 25.2 %scatter_fusion = s32[16,96]{1,0:T(8,128)S(1)} fusion(s32[16,96]{1,0:T(8,128)S(1)} %broadcast_in_dim.12, s32[512]{0:T(512)S(1)} %bitcast.82, s32[512]{0:T(512)S(1)} %add_select_fusion.1), kind=kCustom, calls=%fused_computation | custom fusion | bytes 10240 | tf_op jit(solution)/shard_map/scatter | solution.py:47
  116.8 0.0 all-to-all-done.1
  116.9 14.0 %all_to_all.18 = s32[16,1,96]{2,1,0:T(1,128)S(1)} all-to-all(s32[16,1,96]{2,1,0:T(1,128)S(1)} %bitcast.75), channel_id=1, replica_groups=mesh['movie'=16,'user'=2] {'movie'}, dimensions={0} | all-to-all | bytes 12288 | tf_op jit(solution)/shard_map/all_to_all | solution.py:53
  130.9 6.6 %convert_reduce_fusion.1 = (f32[5600]{0:T(1024)S(1)}, bf16[16,4,5600]{2,1,0:T(4,128)(2,1)S(1)}) fusion(s32[16,96]{1,0:T(8,128)S(1)} %bitcast.85, s32[16,96]{1,0:T(8,128)S(1)} %bitcast.86), kind=kOutput, calls=%fused_computation.12 | convolution fusion | flops 78490144 | bytes 751488 | tf_op jit(solution)/shard_map/ncu,ncj->nuj/dot_general | solution.py:62
  137.5 0.3 convert_element_type.42
  137.8 0.0 copy-start.1
  137.8 0.0 copy-start.3
  137.8 7.3 %fusion.24 = f32[64,1024]{1,0:T(8,128)} fusion(bf16[64,5600]{1,0:T(8,128)(2,1)S(1)} %convert_element_type.42, bf16[5600,1024]{1,0:T(8,128)(2,1)} %bitcast.77), kind=kOutput, calls=%fused_computation.65 | convolution fusion | flops 734003200 | bytes 12447744 | tf_op jit(solution)/shard_map/dot_general | solution.py:23
  145.1 0.0 copy-done.1
  145.1 0.0 all-reduce.4.cloned.1.call-update
  145.2 0.2 all-reduce.6.cloned.1.call-start
  145.4 0.0 copy-done.3
  145.4 0.1 add.96
  145.5 0.9 convert_element_type.45
  146.4 0.0 copy-start.4
  146.4 0.8 reduce_sum.71
  147.2 1.1 mul.26
  148.3 2.7 mul.27
  151.1 98.4 %all-reduce.4.cloned.1.call-done = f32[64,1024]{1,0:T(8,128)} async-done(((f32[64,1024]{1,0:T(8,128)}), f32[64,1024]{1,0:T(8,128)}) %all-reduce.4.cloned.1.call-update) | async-done | bytes 262160 | tf_op jit(solution)/shard_map/psum | solution.py:24
  249.4 0.0 copy-done.4
  249.4 1.0 add_divide_fusion.1
  250.5 0.0 slice-start.1
  250.5 0.0 slice-start.2
  250.5 11.1 %fusion.9 = f32[5600,1024]{1,0:T(8,128)} fusion(bf16[64,5600]{1,0:T(8,128)(2,1)} %copy-done.1, f32[64,1024]{1,0:T(8,128)S(1)} %add_divide_fusion.1), kind=kOutput, calls=%fused_computation.22 | convolution fusion | flops 734068736 | bytes 23916544 | tf_op jit(solution)/shard_map/dot_general | solution.py:76
  261.6 0.0 slice-done
  261.7 0.0 slice-done.1
  261.7 0.0 slice-done.2
  261.7 4.7 convolution_add_fusion
  266.4 1.9 reshape.182
  268.3 0.7 reduce_max.9
  269.0 1.0 fusion.3
  270.0 0.8 fusion.4
  270.8 7.1 %convolution_bitcast_fusion = f32[64,1024]{1,0:T(8,128)} fusion(bf16[5,1120,1024]{2,1,0:T(8,128)(2,1)} %param.9, bf16[64,5,1120]{2,1,0:T(8,128)(2,1)S(1)} %fusion.4), kind=kOutput, calls=%fused_computation.15 | convolution fusion | flops 734003200 | bytes 12447744 | tf_op jit(solution)/shard_map/dot_general | solution.py:23
  277.9 0.0 all-reduce.6.cloned.1.call-update
  277.9 0.3 all-reduce.8.cloned.1.call-start
  278.2 0.2 sub.51
  278.3 1.6 sub.52
  280.0 1.6 div.54
  281.5 3.0 div.55
  284.5 0.0 copy-done
  284.5 3.0 convert_reduce_fusion
  287.5 97.3 %all-reduce.6.cloned.1.call-done = f32[64,1024]{1,0:T(8,128)} async-done(((f32[64,1024]{1,0:T(8,128)}), f32[64,1024]{1,0:T(8,128)}) %all-reduce.6.cloned.1.call-update) | async-done | bytes 262160 | tf_op jit(solution)/shard_map/psum | solution.py:24
  384.8 1.0 add_divide_fusion
  385.8 15.5 %convolution_subtract_fusion = f32[5600,1024]{1,0:T(8,128)} fusion(f32[5600,1024]{1,0:T(8,128)} %fusion.9, bf16[64,5600]{1,0:T(8,128)(2,1)} %get-tuple-element.7, f32[64,1024]{1,0:T(8,128)S(1)} %add_divide_fusion), kind=kOutput, calls=%fused_computation.5 | convolution fusion | flops 739803136 | bytes 46854144 | tf_op jit(solution)/shard_map/dot_general | solution.py:79
  401.3 0.0 all-reduce.8.cloned.1.call-update
  401.3 0.1 reshape.184
  401.4 4.0 psum.31
  405.4 0.6 subtract_reduce_fusion
  406.0 39.9 %all-gather = f32[32768]{0:T(1024)S(1)} all-gather(f32[1024]{0:T(1024)S(1)} %get-tuple-element.4), channel_id=2, replica_groups=mesh['movie'=16,'user'=2] {'movie','user'}, dimensions={0}, use_global_device_ids=true | all-gather | bytes 135168 | tf_op jit(solution)/shard_map/all_gather | solution.py:87
  445.9 0.6 reduce_sum.75
  446.5 29.2 %all-reduce.8.cloned.1.call-done = f32[5,1120,1024]{2,1,0:T(8,128)} async-done(((f32[5,1120,1024]{2,1,0:T(8,128)}), f32[5,1120,1024]{2,1,0:T(8,128)}) %all-reduce.8.cloned.1.call-update) | async-done | bytes 22937616 | tf_op jit(solution)/shard_map/psum | solution.py:85
  475.8 16.5 %copy.41 = f32[5,1120,1024]{2,1,0:T(8,128)} copy(f32[5,1120,1024]{2,1,0:T(8,128)} %all-reduce.8.cloned.1.call-done) | data formatting | bytes 45875200
  (13 shorter events, 0.1 us)
Async XLA Ops:
  83.2 33.7 %all-to-all-start.1 = ((s32[16,1,96]{2,1,0:T(1,128)}), s32[16,1,96]{2,1,0:T(1,128)S(1)}, u32[]{:S(2)}, u32[]{:S(2)}) async-start(s32[16,1,96]{2,1,0:T(1,128)} %bitcast.13), calls=%async_computation.1 | async-start | bytes 16384 | tf_op jit(solution)/shard_map/all_to_all | solution.py:54
  91.6 157.9 %all-reduce.4.cloned.1.call-start = ((), (), s32[]{:S(2)}) async-start(), calls=%async_computation.2 | async-start | bytes 524288 | tf_op jit(solution)/shard_map/psum | solution.py:24
  137.8 7.4 %copy-start.1 = (bf16[64,5600]{1,0:T(8,128)(2,1)}, bf16[64,5600]{1,0:T(8,128)(2,1)S(1)}, u32[]{:S(2)}) copy-start(bf16[64,5600]{1,0:T(8,128)(2,1)S(1)} %convert_element_type.42) | copy-start | bytes 2150404
  137.8 7.6 %copy-start.3 = (f32[5,1120]{1,0:T(8,128)S(1)}, f32[5,1120]{1,0:T(8,128)}, u32[]{:S(2)}) copy-start(f32[5,1120]{1,0:T(8,128)} %param.10) | copy-start | bytes 67204
  145.2 239.6 %all-reduce.6.cloned.1.call-start = ((), (), s32[]{:S(2)}) async-start(), calls=%async_computation.3 | async-start | bytes 524288 | tf_op jit(solution)/shard_map/psum | solution.py:24
  146.4 103.1 %copy-start.4 = (f32[1024]{0:T(1024)S(1)}, f32[1024]{0:T(1024)}, u32[]{:S(2)}) copy-start(f32[1024]{0:T(1024)} %param.11) | copy-start | bytes 12292
  148.3 113.3 %slice-start = ((s8[11468800]{0:T(1024)(128)(4,1)}), s8[3080192]{0:T(1024)(128)(4,1)S(1)}, s32[]{:S(2)}) async-start(s8[11468800]{0:T(1024)(128)(4,1)} %bitcast.78), calls=%async_computation.5 | async-start | bytes 6160384
  250.5 11.2 %slice-start.1 = ((s8[11468800]{0:T(1024)(128)(4,1)}), s8[4194304]{0:T(1024)(128)(4,1)S(1)}, s32[]{:S(2)}) async-start(s8[11468800]{0:T(1024)(128)(4,1)} %bitcast.78), calls=%async_computation.6 | async-start | bytes 8388608
  250.5 11.2 %slice-start.2 = ((s8[11468800]{0:T(1024)(128)(4,1)}), s8[4194304]{0:T(1024)(128)(4,1)S(1)}, s32[]{:S(2)}) async-start(s8[11468800]{0:T(1024)(128)(4,1)} %bitcast.78), calls=%async_computation.7 | async-start | bytes 8388608
  277.9 197.9 %all-reduce.8.cloned.1.call-start = ((), (), s32[]{:S(2)}) async-start(), calls=%async_computation.4 | async-start | bytes 45875200 | tf_op jit(solution)/shard_map/psum | solution.py:85
  281.5 3.0 copy-start
  281.5 3.0 copy-start.2
Sparse Core Ops, SparseCore 0:
  145.3 104.1 all-reduce.3
  278.0 106.6 all-reduce.5
  401.4 74.3 all-reduce.7
